TPU v7x, 32 devices: a whole 2x2x4 slice. The times are simulated.
32 devices in a mesh: row: 4 (over y, core), col: 4 (over z), dp: 2 (over x).
Axes of the slice: x: 2, y: 2, z: 4, core: 2. Of those that a mesh axis runs over, the one named last changes fastest.
Arguments:
- observed: bfloat16 [1024, 2048], P(('row', 'dp'), 'col'), may hold values from -6 to 6
- next_observed: bfloat16 [1024, 2048], P(('row', 'dp'), 'col'), may hold values from -6 to 6
- actions: bfloat16 [1024, 128], P(('row', 'dp')), may hold values from -1 to 1
- next_mean: bfloat16 [1024, 128], P(('row', 'dp')), may hold values from -1.1953125 to 1.1953125
- policy_noise: float32 [1024, 128], P(('row', 'dp')), may hold values from -1.5 to 1.5
- rewards: bfloat16 [1024], P(('row', 'dp')), may hold values from -5 to 5
- discounts: bfloat16 [1024], P(('row', 'dp')), may hold values from 0.5 to 0.98828125
- actor_flags: int32 [1024], P(('row', 'dp')), may hold values 0 or 1
- critic_in: float32 [2, 2048, 2048], P(None, 'col', 'row'), may hold values from -0.125 to 0.125
- critic_act: float32 [2, 128, 2048], P(None, None, 'col'), may hold values from -0.5 to 0.5
- critic_head: float32 [2, 2048], P(None, 'row'), may hold values from -0.125 to 0.125
- target_in: float32 [2, 2048, 2048], P(None, 'col', 'row'), may hold values from -0.125 to 0.125
- target_act: float32 [2, 128, 2048], P(None, None, 'col'), may hold values from -0.5 to 0.5
- target_head: float32 [2, 2048], P(None, 'row'), may hold values from -0.125 to 0.125
Outputs:
- new_in: float32 [2, 2048, 2048], P(None, 'col', 'row')
- new_act: float32 [2, 128, 2048], P(None, None, 'col')
- new_head: float32 [2, 2048], P(None, 'row')
- new_target_in: float32 [2, 2048, 2048], P(None, 'col', 'row')
- new_target_act: float32 [2, 128, 2048], P(None, None, 'col')
- new_target_head: float32 [2, 2048], P(None, 'row')
- temporal_errors: float32 [2, 1024], P(None, ('row', 'dp'))
- action_slope: float32 [1024, 128], P(('row', 'dp'))
All inputs are finite; a program needn't handle non-finite values. No bound on the sum of `actor_flags` on one device may be relied on, other than what follows from the above.
Results may differ from a plain program's by a relative error of at most 0.008.
Values may be sent and summed in bfloat16 or wider, within the bound.
A program may use at most 128 MiB of HBM per device.

v0:
```python
import jax
import jax.numpy as jnp
from jax import lax
from jax.sharding import PartitionSpec as P

noise_clip = 0.5
matrix_rate = 0.004
head_rate = 0.0001
blend_rate = 0.005


def silu_slope(preact):
    sigma = jax.nn.sigmoid(preact)
    return sigma * (1.0 + preact * (1.0 - sigma))


def embed(states, moves, weight_act):
    summed = states.astype(jnp.float32) + jnp.dot(
        moves, weight_act.astype(jnp.bfloat16), preferred_element_type=jnp.float32
    )
    return summed.astype(jnp.bfloat16)


def contract_rows(left, right):
    return lax.dot_general(
        left, right, (((0,), (0,)), ((), ())), preferred_element_type=jnp.float32
    )


def on_device(
    observed,
    next_observed,
    actions,
    next_mean,
    policy_noise,
    rewards,
    discounts,
    actor_flags,
    critic_in,
    critic_act,
    critic_head,
    target_in,
    target_act,
    target_head,
):
    noisy = jnp.clip(
        next_mean.astype(jnp.float32) + jnp.clip(policy_noise, -noise_clip, noise_clip), -1.0, 1.0
    ).astype(jnp.bfloat16)
    states, next_states, moves, next_moves, group_rewards, group_discounts = (
        lax.all_gather(observed, "row", axis=0, tiled=True),
        lax.all_gather(next_observed, "row", axis=0, tiled=True),
        lax.all_gather(actions, "row", axis=0, tiled=True),
        lax.all_gather(noisy, "row", axis=0, tiled=True),
        lax.all_gather(rewards, "row", axis=0, tiled=True),
        lax.all_gather(discounts, "row", axis=0, tiled=True),
    )
    inner = [critic_in[which].astype(jnp.bfloat16) for which in range(2)]
    online = [embed(states, moves, critic_act[which]) for which in range(2)]
    shadow = [embed(next_states, next_moves, target_act[which]) for which in range(2)]
    partials = [
        jnp.dot(online[which], inner[which], preferred_element_type=jnp.float32)
        for which in range(2)
    ]
    partials += [
        jnp.dot(
            shadow[which], target_in[which].astype(jnp.bfloat16), preferred_element_type=jnp.float32
        )
        for which in range(2)
    ]
    total_rows = states.shape[0]
    preacts = (
        lax.psum_scatter(partials[0], "col", scatter_dimension=0, tiled=True),
        lax.psum_scatter(partials[1], "col", scatter_dimension=0, tiled=True),
        lax.psum_scatter(partials[2], "col", scatter_dimension=0, tiled=True),
        lax.psum_scatter(partials[3], "col", scatter_dimension=0, tiled=True),
    )
    row_count = total_rows // lax.axis_size("col")
    first_row = lax.axis_index("col") * row_count
    share_rewards = lax.dynamic_slice_in_dim(group_rewards, first_row, row_count).astype(
        jnp.float32
    )
    share_discounts = lax.dynamic_slice_in_dim(group_discounts, first_row, row_count).astype(
        jnp.float32
    )
    heads = [critic_head[0], critic_head[1], target_head[0], target_head[1]]
    hiddens = [jax.nn.silu(preacts[which]) for which in range(4)]
    value_terms = [
        jnp.dot(hiddens[which], heads[which], precision=lax.Precision.HIGHEST) for which in range(4)
    ]
    values = lax.psum((value_terms[0], value_terms[1], value_terms[2], value_terms[3]), "row")
    goal = share_rewards + share_discounts * jnp.minimum(values[2], values[3])
    errors = [values[0] - goal, values[1] - goal]
    slopes = [
        (heads[which] * silu_slope(preacts[which])).astype(jnp.bfloat16) for which in range(2)
    ]
    head_grads = [
        jnp.dot(2.0 * errors[which], hiddens[which], precision=lax.Precision.HIGHEST)
        for which in range(2)
    ]
    slopes = list(
        (
            lax.all_gather(slopes[0], "col", axis=0, tiled=True),
            lax.all_gather(slopes[1], "col", axis=0, tiled=True),
        )
    )
    errors = list(
        (
            lax.all_gather(errors[0], "col", axis=0, tiled=True),
            lax.all_gather(errors[1], "col", axis=0, tiled=True),
        )
    )
    head_grads = list(lax.psum((head_grads[0], head_grads[1]), "col"))
    deltas = [
        (2.0 * errors[which][:, None] * slopes[which].astype(jnp.float32)).astype(jnp.bfloat16)
        for which in range(2)
    ]
    back_terms = [
        lax.dot_general(
            slopes[which],
            inner[which],
            (((1,), (1,)), ((), ())),
            preferred_element_type=jnp.float32,
        )
        for which in range(2)
    ]
    grad_ins = [contract_rows(online[which], deltas[which]) for which in range(2)]
    own_rows = observed.shape[0]
    own_first = lax.axis_index("row") * own_rows
    own_errors = [
        lax.dynamic_slice_in_dim(errors[which], own_first, own_rows) for which in range(2)
    ]
    backs = lax.psum((back_terms[0], back_terms[1]), "row")
    grad_embedded = [
        (2.0 * errors[which][:, None] * backs[which]).astype(jnp.bfloat16) for which in range(2)
    ]
    grad_acts = [contract_rows(moves, grad_embedded[which]) for which in range(2)]
    mine = lax.dynamic_slice_in_dim(backs[0], own_first, own_rows).astype(jnp.bfloat16)
    push_term = lax.dot_general(
        mine,
        critic_act[0].astype(jnp.bfloat16),
        (((1,), (1,)), ((), ())),
        preferred_element_type=jnp.float32,
    )
    action_slope = lax.psum(push_term, "col") * actor_flags.astype(jnp.float32)[:, None]
    temporal_errors = jnp.stack(own_errors)
    olds = [
        critic_in[0],
        critic_in[1],
        critic_act[0],
        critic_act[1],
        critic_head[0],
        critic_head[1],
    ]
    rates = [matrix_rate, matrix_rate, matrix_rate, matrix_rate, head_rate, head_rate]
    summed = lax.psum(
        (grad_ins[0], grad_ins[1], grad_acts[0], grad_acts[1], head_grads[0], head_grads[1]), "dp"
    )
    fresh = [olds[which] - rates[which] * summed[which] for which in range(6)]
    new_in = jnp.stack([fresh[0], fresh[1]])
    new_act = jnp.stack([fresh[2], fresh[3]])
    new_head = jnp.stack([fresh[4], fresh[5]])
    new_target_in = blend_rate * new_in + (1.0 - blend_rate) * target_in
    new_target_act = blend_rate * new_act + (1.0 - blend_rate) * target_act
    new_target_head = blend_rate * new_head + (1.0 - blend_rate) * target_head
    return (
        new_in,
        new_act,
        new_head,
        new_target_in,
        new_target_act,
        new_target_head,
        temporal_errors,
        action_slope,
    )


def solution(mesh):
    return jax.shard_map(
        on_device,
        mesh=mesh,
        in_specs=(
            P(("row", "dp"), "col"),
            P(("row", "dp"), "col"),
            P(("row", "dp"), None),
            P(("row", "dp"), None),
            P(("row", "dp"), None),
            P(("row", "dp")),
            P(("row", "dp")),
            P(("row", "dp")),
            P(None, "col", "row"),
            P(None, None, "col"),
            P(None, "row"),
            P(None, "col", "row"),
            P(None, None, "col"),
            P(None, "row"),
        ),
        out_specs=(
            P(None, "col", "row"),
            P(None, None, "col"),
            P(None, "row"),
            P(None, "col", "row"),
            P(None, None, "col"),
            P(None, "row"),
            P(None, ("row", "dp")),
            P(("row", "dp"), None),
        ),
        check_vma=False,
    )
```

profile of v0, /device:TPU:1, one launch (start us, length us, event | category | flops | bytes accessed | tf_op | source)
XLA Modules:
  0.0 337.1 jit_solution(6324428387453273612)
XLA Ops:
  7.2 6.7 %all_gather.31 = bf16[512,128]{1,0:T(8,128)(2,1)S(1)} all-gather(bf16[128,128]{1,0:T(8,128)(2,1)} %param.16), channel_id=1, replica_groups=mesh['row'=4,'col'=4,'dp'=2] {'row'}, dimensions={0}, use_global_device_ids=true | all-gather | bytes 163840 | tf_op jit(solution)/shard_map/all_gather | solution.py:52
  14.0 7.8 %all_gather.30 = bf16[512,512]{1,0:T(8,128)(2,1)S(1)} all-gather(bf16[128,512]{1,0:T(8,128)(2,1)} %param.14), channel_id=1, replica_groups=mesh['row'=4,'col'=4,'dp'=2] {'row'}, dimensions={0}, use_global_device_ids=true | all-gather | bytes 655360 | tf_op jit(solution)/shard_map/all_gather | solution.py:50
  21.7 1.1 fusion.69
  22.8 0.1 copy.37
  22.9 0.3 fusion
  23.2 0.8 copy-done.2
  24.0 1.5 fusion.29
  25.5 0.1 copy.38
  25.7 0.3 fusion.3
  26.0 0.8 copy-done.3
  26.8 1.4 fusion.31
  28.4 2.7 convert.9
  31.1 5.4 %all_gather.35 = bf16[512,128]{1,0:T(8,128)(2,1)S(1)} all-gather(bf16[128,128]{1,0:T(8,128)(2,1)S(1)} %clamp_convert_fusion), channel_id=1, replica_groups=mesh['row'=4,'col'=4,'dp'=2] {'row'}, dimensions={0}, use_global_device_ids=true | all-gather | bytes 163840 | tf_op jit(solution)/shard_map/all_gather | solution.py:53
  36.5 7.3 %all_gather.34 = bf16[512,512]{1,0:T(8,128)(2,1)S(1)} all-gather(bf16[128,512]{1,0:T(8,128)(2,1)S(1)} %copy-done.11), channel_id=1, replica_groups=mesh['row'=4,'col'=4,'dp'=2] {'row'}, dimensions={0}, use_global_device_ids=true | all-gather | bytes 655360 | tf_op jit(solution)/shard_map/all_gather | solution.py:51
  43.8 2.6 fusion.5
  46.5 2.6 fusion.4
  49.1 5.1 %all-gather = bf16[4,1,128]{2,1,0:T(2,128)(2,1)S(1)} all-gather(bf16[1,1,128]{2,1,0:T(2,128)(2,1)S(1)} %bitcast.154), channel_id=1, replica_groups=mesh['row'=4,'col'=4,'dp'=2] {'row'}, dimensions={0}, use_global_device_ids=true | all-gather | bytes 1280 | tf_op jit(solution)/shard_map/all_gather | solution.py:54
  54.2 0.6 reduce
  54.8 5.0 %all-gather.1 = bf16[4,1,128]{2,1,0:T(2,128)(2,1)S(1)} all-gather(bf16[1,1,128]{2,1,0:T(2,128)(2,1)S(1)} %bitcast.155), channel_id=1, replica_groups=mesh['row'=4,'col'=4,'dp'=2] {'row'}, dimensions={0}, use_global_device_ids=true | all-gather | bytes 1280 | tf_op jit(solution)/shard_map/all_gather | solution.py:55
  59.8 0.6 reduce.1
  60.4 1.1 multiply_convert_fusion.9
  61.5 21.9 %all_gather.37 = bf16[512,512]{1,0:T(8,128)(2,1)S(1)} all-gather(bf16[128,512]{1,0:T(8,128)(2,1)S(1)} %multiply_convert_fusion.9), channel_id=1, replica_groups=mesh['row'=4,'col'=4,'dp'=2] {'col'}, dimensions={0}, use_global_device_ids=true | all-gather | bytes 655360 | tf_op jit(solution)/shard_map/all_gather | solution.py:102
  83.4 7.1 %reduce-scatter.11.cloned.1.call-done = f32[128,512]{1,0:T(8,128)} async-done(((f32[512,512]{1,0:T(8,128)}), f32[128,512]{1,0:T(8,128)}) %reduce-scatter.11.cloned.1.call-update) | async-done | bytes 262160 | tf_op jit(solution)/shard_map/reduce_scatter | solution.py:73
  90.5 1.1 multiply_convert_fusion.8
  91.5 14.5 %all_gather.39 = bf16[512,512]{1,0:T(8,128)(2,1)S(1)} all-gather(bf16[128,512]{1,0:T(8,128)(2,1)S(1)} %multiply_convert_fusion.8), channel_id=1, replica_groups=mesh['row'=4,'col'=4,'dp'=2] {'col'}, dimensions={0}, use_global_device_ids=true | all-gather | bytes 655360 | tf_op jit(solution)/shard_map/all_gather | solution.py:103
  106.0 1.4 fusion.28
  107.5 1.5 fusion.30
  109.0 1.8 convolution_bitcast_fusion.5
  110.8 1.8 convolution_bitcast_fusion.2
  112.7 9.6 %reduce-scatter.7.cloned.1.call-done = f32[128,512]{1,0:T(8,128)} async-done(((f32[512,512]{1,0:T(8,128)}), f32[128,512]{1,0:T(8,128)}) %reduce-scatter.7.cloned.1.call-update) | async-done | bytes 262160 | tf_op jit(solution)/shard_map/reduce_scatter | solution.py:74
  122.3 1.8 convolution_bitcast_fusion.4
  124.1 27.2 %reduce-scatter.9.cloned.1.call-done = f32[128,512]{1,0:T(8,128)} async-done(((f32[512,512]{1,0:T(8,128)}), f32[128,512]{1,0:T(8,128)}) %reduce-scatter.9.cloned.1.call-update) | async-done | bytes 262160 | tf_op jit(solution)/shard_map/reduce_scatter | solution.py:75
  151.3 1.8 convolution_bitcast_fusion.3
  153.1 6.8 %all-reduce.1 = (f32[128]{0:T(128)}, f32[128]{0:T(128)}, f32[128]{0:T(128)}, f32[128]{0:T(128)S(1)}) all-reduce(f32[128]{0:T(128)} %convolution_bitcast_fusion.2, f32[128]{0:T(128)} %convolution_bitcast_fusion.4, f32[128]{0:T(128)} %convolution_bitcast_fusion.3, f32[128]{0:T(128)S(1)} %copy-done.21), channel_id=1, replica_groups=mesh['row'=4,'col'=4,'dp'=2] {'row'}, use_global_device_ids=true, to_apply=%region_8.9 | all-reduce | flops 512 | bytes 4096 | tf_op jit(solution)/shard_map/psum | solution.py:90
  159.9 0.9 subtract_bitcast_fusion.1
  160.8 0.7 subtract_bitcast_fusion
  161.4 6.5 %all-gather.3 = f32[4,1,128]{2,1,0:T(1,128)S(1)} all-gather(f32[1,1,128]{2,1,0:T(1,128)S(1)} %subtract_bitcast_fusion), channel_id=1, replica_groups=mesh['row'=4,'col'=4,'dp'=2] {'col'}, dimensions={0}, use_global_device_ids=true | all-gather | bytes 2560 | tf_op jit(solution)/shard_map/all_gather | solution.py:109
  167.9 7.4 %all-gather.2 = f32[4,1,128]{2,1,0:T(1,128)S(1)} all-gather(f32[1,1,128]{2,1,0:T(1,128)S(1)} %get-tuple-element.50), channel_id=1, replica_groups=mesh['row'=4,'col'=4,'dp'=2] {'col'}, dimensions={0}, use_global_device_ids=true | all-gather | bytes 2560 | tf_op jit(solution)/shard_map/all_gather | solution.py:108
  175.3 0.6 copy-done.15
  175.9 2.6 fusion.8
  178.5 1.5 fusion.9
  180.0 23.7 %all-reduce.11.cloned.1.call-done = (f32[512,512]{1,0:T(8,128)}, f32[512,512]{1,0:T(8,128)}) async-done(((f32[512,512]{1,0:T(8,128)}, f32[512,512]{1,0:T(8,128)}), (f32[512,512]{1,0:T(8,128)}, f32[512,512]{1,0:T(8,128)})) %all-reduce.11.cloned.1.call-update) | async-done | bytes 2097168 | tf_op jit(solution)/shard_map/psum | solution.py:132
  203.7 2.3 convolution_bitcast_fusion.1
  206.1 1.8 fusion.32
  207.9 2.4 convolution_bitcast_fusion
  210.4 1.0 copy.34
  211.4 0.3 fusion.35
  211.7 1.2 fusion.38
  212.9 9.8 %all-reduce = (f32[512]{0:T(512)S(1)}, f32[512]{0:T(512)S(1)}) all-reduce(f32[512]{0:T(512)S(1)} %bitcast.153, f32[512]{0:T(512)S(1)} %bitcast.152), channel_id=1, replica_groups=mesh['row'=4,'col'=4,'dp'=2] {'col'}, use_global_device_ids=true, to_apply=%region_16.17 | all-reduce | flops 1024 | bytes 8192 | tf_op jit(solution)/shard_map/psum | solution.py:112
  222.7 3.8 %all-reduce.3 = (f32[512]{0:T(512)S(1)}, f32[512]{0:T(512)S(1)}) all-reduce(f32[512]{0:T(512)S(1)} %get-tuple-element.32, f32[512]{0:T(512)S(1)} %get-tuple-element.33), channel_id=1, replica_groups=mesh['row'=4,'col'=4,'dp'=2] {'dp'}, use_global_device_ids=true, to_apply=%region_17.18 | all-reduce | flops 1024 | bytes 8192 | tf_op jit(solution)/shard_map/psum | solution.py:155
  226.4 0.8 dynamic-slice_bitcast_fusion
  227.2 0.8 dynamic-slice_bitcast_fusion.1
  228.0 0.6 pad_maximum_fusion.3
  228.5 0.6 multiply_add_fusion.2
  229.1 11.4 %all-reduce.9.cloned.1.call-done = f32[128,128]{1,0:T(8,128)} async-done(((f32[128,128]{1,0:T(8,128)}), f32[128,128]{1,0:T(8,128)}) %all-reduce.9.cloned.1.call-update) | async-done | bytes 65552 | tf_op jit(solution)/shard_map/psum | solution.py:144
  240.6 1.6 broadcast_multiply_fusion
  242.1 77.5 %all-reduce.13.cloned.1.call-done = (f32[512,512]{1,0:T(8,128)}, f32[512,512]{1,0:T(8,128)}, f32[128,512]{0,1:T(8,128)}, f32[128,512]{0,1:T(8,128)}) async-done(((f32[512,512]{1,0:T(8,128)}, f32[512,512]{1,0:T(8,128)}, f32[128,512]{0,1:T(8,128)}, f32[128,512]{0,1:T(8,128)}), (f32[512,512]{1,0:T(8,128)}, f32[512,512]{1,0:T(8,128)}, f32[128,512]{0,1:T(8,128)}, ...) | async-done | bytes 2621456 | tf_op jit(solution)/shard_map/psum | solution.py:155
  319.6 1.0 fusion.15
  320.6 1.0 fusion.14
  321.6 0.9 multiply_add_fusion.1
  322.5 2.0 copy.36
  324.5 1.0 copy.35
  325.5 2.2 fusion.7
  327.7 2.5 multiply_add_fusion
  (76 shorter events, 0.6 us)
Async XLA Ops:
  7.2 16.8 %copy-start = (f32[2,512,512]{2,1,0:T(8,128)S(1)}, f32[2,512,512]{2,1,0:T(8,128)}, u32[]{:S(2)}) copy-start(f32[2,512,512]{2,1,0:T(8,128)} %param.22) | copy-start | bytes 6291460
  7.2 53.2 %reduce-scatter.5.cloned.1.call-start = ((), (), s32[]{:S(2)}) async-start(), calls=%async_computation.4 | async-start | bytes 1310720 | tf_op jit(solution)/shard_map/reduce_scatter | solution.py:72
  23.2 0.8 copy-start.2
  25.5 65.0 %reduce-scatter.11.cloned.1.call-start = ((), (), s32[]{:S(2)}) async-start(), calls=%async_computation.7 | async-start | bytes 1310720 | tf_op jit(solution)/shard_map/reduce_scatter | solution.py:73
  25.7 2.6 copy-start.5
  26.0 0.8 copy-start.3
  26.8 1.5 copy-start.7
  28.2 8.3 %copy-start.11 = (bf16[128,512]{1,0:T(8,128)(2,1)S(1)}, bf16[128,512]{1,0:T(8,128)(2,1)}, u32[]{:S(2)}) copy-start(bf16[128,512]{1,0:T(8,128)(2,1)} %param.15) | copy-start | bytes 393220
  28.2 94.0 %reduce-scatter.7.cloned.1.call-start = ((), (), s32[]{:S(2)}) async-start(), calls=%async_computation.5 | async-start | bytes 1310720 | tf_op jit(solution)/shard_map/reduce_scatter | solution.py:74
  28.3 2.8 copy-start.12
  28.3 2.8 copy-start.13
  46.4 2.7 copy-start.19
  46.4 8.4 %copy-start.20 = (bf16[128]{0:T(256)(128)(2,1)S(1)}, bf16[128]{0:T(256)(128)(2,1)}, u32[]{:S(2)}) copy-start(bf16[128]{0:T(256)(128)(2,1)} %param.20) | copy-start | bytes 772
  46.4 14.0 %copy-start.16 = (f32[2,512]{1,0:T(2,128)S(1)}, f32[2,512]{1,0:T(2,128)}, u32[]{:S(2)}) copy-start(f32[2,512]{1,0:T(2,128)} %param.24) | copy-start | bytes 12292
  46.4 104.9 %reduce-scatter.9.cloned.1.call-start = ((), (), s32[]{:S(2)}) async-start(), calls=%async_computation.6 | async-start | bytes 1310720 | tf_op jit(solution)/shard_map/reduce_scatter | solution.py:75
  49.1 154.6 %all-reduce.11.cloned.1.call-start = ((), (), s32[]{:S(2)}) async-start(), calls=%async_computation.9 | async-start | bytes 4194304 | tf_op jit(solution)/shard_map/psum | solution.py:132
  108.9 13.3 %copy-start.17 = (f32[2,512]{1,0:T(2,128)S(1)}, f32[2,512]{1,0:T(2,128)}, u32[]{:S(2)}) copy-start(f32[2,512]{1,0:T(2,128)} %param.27) | copy-start | bytes 12292
  109.0 131.6 %all-reduce.9.cloned.1.call-start = ((), (), s32[]{:S(2)}) async-start(), calls=%async_computation.8 | async-start | bytes 131072 | tf_op jit(solution)/shard_map/psum | solution.py:144
  112.7 40.5 %copy-start.21 = (f32[128]{0:T(128)S(1)}, f32[128]{0:T(128)}, u32[]{:S(2)}) copy-start(f32[128]{0:T(128)} %convolution_bitcast_fusion.5) | copy-start | bytes 1540
  159.9 0.9 copy-start.22
  159.9 18.6 %copy-start.4 = (bf16[512,512]{1,0:T(8,128)(2,1)S(1)}, bf16[512,512]{1,0:T(8,128)(2,1)}, u32[]{:S(2)}) copy-start(bf16[512,512]{1,0:T(8,128)(2,1)} %copy-done.3) | copy-start | bytes 1572868
  160.8 14.6 %copy-start.24 = (f32[128]{0:T(128)}, f32[128]{0:T(128)S(1)}, u32[]{:S(2)}) copy-start(f32[128]{0:T(128)S(1)} %get-tuple-element.51) | copy-start | bytes 1540
  167.9 7.4 %copy-start.14 = (f32[4,1,128]{2,1,0:T(1,128)}, f32[4,1,128]{2,1,0:T(1,128)S(1)}, u32[]{:S(2)}) copy-start(f32[4,1,128]{2,1,0:T(1,128)S(1)} %all-gather.3) | copy-start | bytes 6148
  175.3 0.6 copy-start.15
  207.8 2.5 copy-start.8
  207.8 111.8 %all-reduce.13.cloned.1.call-start = ((), (), s32[]{:S(2)}) async-start(), calls=%async_computation.10 | async-start | bytes 5242880 | tf_op jit(solution)/shard_map/psum | solution.py:155
  210.3 1.1 copy-start.26
  210.3 1.1 copy-start.10
  210.3 1.1 copy-start.23
  210.3 1.1 copy-start.25
  210.3 1.4 copy-start.27
  210.3 18.2 %copy-start.18 = (f32[2,512]{1,0:T(2,128)S(1)}, f32[2,512]{1,0:T(2,128)}, u32[]{:S(2)}) copy-start(f32[2,512]{1,0:T(2,128)} %param.27) | copy-start | bytes 12292
  210.3 110.2 %copy-start.6 = (f32[1,128,512]{1,2,0:T(8,128)S(1)}, f32[1,128,512]{1,2,0:T(8,128)}, u32[]{:S(2)}) copy-start(f32[1,128,512]{1,2,0:T(8,128)} %copy-done.5) | copy-start | bytes 786436
  211.4 110.2 %copy-start.9 = (f32[2,128,512]{1,2,0:T(8,128)S(1)}, f32[2,128,512]{1,2,0:T(8,128)}, u32[]{:S(2)}) copy-start(f32[2,128,512]{1,2,0:T(8,128)} %copy.34) | copy-start | bytes 1572868
  325.5 2.2 copy-start.1
Sparse Core Ops, SparseCore 0:
  25.6 27.6 reduce-scatter.4
  56.2 34.2 reduce-scatter.10
  92.8 29.4 reduce-scatter.6
  124.4 26.8 reduce-scatter.8
  153.6 50.0 all-reduce.10
  208.0 32.5 all-reduce.8
  243.6 75.9 all-reduce.12
where the time goes:
time: 339 us; the launch traced here: 337 us
  waiting for transfers between devices  157 us (46%)
  blocking collectives  108 us (32%)
  matrix products  31 us (9%)
  other arithmetic  17.9 us (5%)
  between operations  14.4 us (4%)
  local copies, waits for them, and re-layouts  9.12 us (3%)
    psum x1, waiting for transfers between devices, on_device(): lax.psum((grad_ins[0], grad_ins[1], grad_acts[0], grad_acts[1], head_grad...  77.5 us
    reduce_scatter x1, waiting for transfers between devices, on_device(): lax.psum_scatter(partials[3], 'col', scatter_dimension=0, tiled=True)  27.2 us
    psum x1, waiting for transfers between devices, on_device(): backs = lax.psum((back_terms[0], back_terms[1]), 'row')  23.7 us
    all_gather x1, blocking collectives, on_device(): lax.all_gather(slopes[0], 'col', axis=0, tiled=True)  21.9 us
    all_gather x1, blocking collectives, on_device(): lax.all_gather(slopes[1], 'col', axis=0, tiled=True)  14.5 us
    psum x1, waiting for transfers between devices, on_device(): lax.psum(push_term, 'col') * actor_flags.astype(jnp.float32)[:, None]  11.4 us
    psum x1, blocking collectives, on_device(): head_grads = list(lax.psum((head_grads[0], head_grads[1]), 'col'))  9.75 us
    reduce_scatter x1, waiting for transfers between devices, on_device(): lax.psum_scatter(partials[2], 'col', scatter_dimension=0, tiled=True)  9.58 us
  transfers between devices with their start and end apart: 7, of which 6 were waited for; matrix products, arithmetic and copies ran while one was open for 11% of the time, Pallas kernels for 0%

commit v1 on v0

v1 whole, which is shorter than its diff:
```python
import functools

import jax
import jax.numpy as jnp
from jax import lax
from jax.experimental import pallas as pl
from jax.experimental.pallas import tpu as pltpu
from jax.sharding import PartitionSpec as P

noise_clip = 0.5
matrix_rate = 0.004
head_rate = 0.0001
blend_rate = 0.005

f32 = jnp.float32
bf16 = jnp.bfloat16
skew = 3


def kernel(dims, on_own, tg_own, cin, tin, cact, tact, heads, g_in, g_act, g_head, errs_out, push_out,
           w16, a16, on_all, tg_all, emb, slopes, delta, rs_out, rs_in, hidden, vals, vt_own, vt_in,
           errs, gh, epad, ga_own, ga_out, ga_in, ga_all, pu_out, pu_in, pz_all,
           on_s, on_r, tg_s, tg_r, fon_s, fon_r, ftg_s, ftg_r, xon_s, xon_r,
           rs_s, rs_r, sl_s, sl_r, xs_s, xs_r, vt_s, vt_r, er_s, er_r, gh_s, gh_r,
           ga_s, ga_r, gb_s, gb_r, pu_s, pu_r, pz_s, pz_r):
    R, C, D, TB, F, H, A = dims
    HI = R // 2
    TC = TB // 2
    row, col, dp = lax.axis_index("row"), lax.axis_index("col"), lax.axis_index("dp")
    hi, lo = row // 2, row % 2
    n = 8 * HI
    m = n // 2

    def copy(src, dst, ssem, rsem, **where):
        return pltpu.make_async_remote_copy(
            src_ref=src, dst_ref=dst, send_sem=ssem, recv_sem=rsem,
            device_id=where, device_id_type=pl.DeviceIdType.MESH)

    plane = [(c, d) for d in range(D) for c in range(C) if c or d]
    barrier = pltpu.get_barrier_semaphore()
    for o in range(1, R):
        pl.semaphore_signal(barrier, inc=1, device_id={"row": (row + o) % R},
                            device_id_type=pl.DeviceIdType.MESH)
    for c, d in plane:
        pl.semaphore_signal(barrier, inc=1,
                            device_id={"col": (col + c) % C, "dp": (dp + d) % D},
                            device_id_type=pl.DeviceIdType.MESH)
    pl.semaphore_wait(barrier, R - 1 + len(plane))

    def on_copy(o):
        to = hi * 2 + (1 - lo) if o == 0 else ((hi + o) % HI) * 2 + lo
        return copy(on_own, on_all.at[dp, row], on_s.at[o], on_r.at[o], row=to)

    def tg_copy(o):
        to = hi * 2 + (1 - lo) if o == 0 else ((hi + o) % HI) * 2 + lo
        return copy(tg_own, tg_all.at[row], tg_s.at[o], tg_r.at[o], row=to)

    for o in range(HI):
        on_copy(o).start()
    for o in range(HI):
        tg_copy(o).start()
    on_all[dp, row] = on_own[...]
    tg_all[row] = tg_own[...]
    for k in range(2):
        w16[k] = cin[k].astype(bf16)
        w16[2 + k] = tin[k].astype(bf16)
        a16[k] = cact[k].astype(bf16)
        a16[2 + k] = tact[k].astype(bf16)

    def fon_copy(o, block):
        return copy(on_all.at[dp, block], on_all.at[dp, block], fon_s.at[o], fon_r.at[o],
                    row=hi * 2 + (1 - lo))

    def ftg_copy(o, block):
        return copy(tg_all.at[block], tg_all.at[block], ftg_s.at[o], ftg_r.at[o],
                    row=hi * 2 + (1 - lo))

    def xon_copy(a, o, block, e):
        return copy(on_all.at[dp, block], on_all.at[dp, block], xon_s.at[a, o, e - 1],
                    xon_r.at[a, o, e - 1], dp=(dp + e) % D)

    def rows_of(d, block):
        return pl.ds(pl.multiple_of((d * R + block) * TB, TB), TB)

    def embed_on(d, block):
        x = on_all[d, block]
        for k in range(2):
            mixed = jnp.dot(x[:, F:], a16[k], preferred_element_type=f32)
            emb[k, rows_of(d, block), :] = (x[:, :F].astype(f32) + mixed).astype(bf16)

    def embed_tg(block):
        x = tg_all[block]
        for k in range(2):
            mixed = jnp.dot(x[:, F:F + A], a16[2 + k], preferred_element_type=f32)
            emb[k, rows_of(D, block), :] = (x[:, :F].astype(f32) + mixed).astype(bf16)

    def prepare(a, i):
        block_of = lambda o: ((hi + o) % HI) * 2 + a
        for o in range(HI):
            block = block_of(o)

            @pl.when(i == 4 * o)
            def _():
                @pl.when(lo == a)
                def _():
                    if o > 0:
                        on_copy(o).wait_recv()
                        fon_copy(o, block).start()

                @pl.when(lo != a)
                def _():
                    if o > 0:
                        fon_copy(o, block).wait_recv()
                    else:
                        on_copy(0).wait_recv()
                for e in range(1, D):
                    xon_copy(a, o, block, e).start()
                embed_on(dp, block)

            @pl.when(i == 4 * (HI + o))
            def _():
                @pl.when(lo == a)
                def _():
                    if o > 0:
                        tg_copy(o).wait_recv()
                        ftg_copy(o, block).start()

                @pl.when(lo != a)
                def _():
                    if o > 0:
                        ftg_copy(o, block).wait_recv()
                    else:
                        tg_copy(0).wait_recv()
                embed_tg(block)

    def place(a, i):
        group = i // (4 * HI)
        o = (i // 4) % HI
        kk = (i // 2) % 2
        half = i % 2
        there = (hi + o) % HI
        return group, kk, half, there, there * 2 + a

    def rs_copy(a, i):
        to = (col + 1) % C if a == 0 else (col + C - 1) % C
        return copy(rs_out.at[a, i], rs_in.at[a, i], rs_s.at[a, i], rs_r.at[a, i], col=to)

    def slope_at(d, kk, block, half):
        start = (d * R + block) * TB + half * TC
        return slopes.at[kk, pl.ds(pl.multiple_of(start, TC), TC), :]

    def sl_copy(a, j):
        _, kk, half, there, block = place(a, j)
        at = slope_at(dp, kk, block, half)
        to = (col + C - 1) % C if a == 0 else (col + 1) % C
        return copy(at, at, sl_s.at[a, j], sl_r.at[a, j], col=to)

    def xs_copy(a, j, e):
        _, kk, half, there, block = place(a, j)
        at = slope_at(dp, kk, block, half)
        return copy(at, at, xs_s.at[a, j, e - 1], xs_r.at[a, j, e - 1], dp=(dp + e) % D)

    lane = lax.broadcasted_iota(jnp.int32, (TC, 128), 1)

    def finish(a, i, pre):
        group, kk, half, there, block = place(a, i)
        sigma = jax.nn.sigmoid(pre)
        hid = pre * sigma
        head = heads[group * 2 + kk]
        value = jnp.sum(hid * head, axis=1, keepdims=True)
        at = pl.ds(pl.multiple_of(there * TB + half * TC, TC), TC)
        vals[at, :] += jnp.where(lane == group * 2 + kk, value, 0.0)

        @pl.when(group == 0)
        def _():
            hidden[kk, at, :] = hid.astype(bf16)
            start = (dp * R + block) * TB + half * TC
            slopes[kk, pl.ds(pl.multiple_of(start, TC), TC), :] = (
                head * (sigma * (1.0 + pre * (1.0 - sigma)))).astype(bf16)
            sl_copy(a, i).start()
            for e in range(1, D):
                xs_copy(a, i, e).start()

    vals[...] = jnp.zeros_like(vals)

    def step(s, carry):
        for a in range(2):
            far = col if a == 0 else C - 1 - col
            i = s - skew * far

            @pl.when((i >= 0) & (i < n))
            def _():
                prepare(a, i)
                group, kk, half, there, block = place(a, i)
                start = (jnp.where(group == 0, dp, D) * R + block) * TB + half * TC

                def partial():
                    left = emb[kk, pl.ds(pl.multiple_of(start, TC), TC), :]
                    return jnp.dot(left, w16[group * 2 + kk], preferred_element_type=f32)

                @pl.when(far == 0)
                def _():
                    rs_out[a, i] = partial().astype(bf16)
                    rs_copy(a, i).start()

                @pl.when((far > 0) & (far < C - 1))
                def _():
                    mine = partial()
                    rs_copy(a, i).wait_recv()
                    rs_out[a, i] = (mine + rs_in[a, i].astype(f32)).astype(bf16)
                    rs_copy(a, i).start()

                @pl.when(far == C - 1)
                def _():
                    mine = partial()
                    rs_copy(a, i).wait_recv()
                    finish(a, i, mine + rs_in[a, i].astype(f32))

            j = s - skew * (2 * (C - 1) - far)

            @pl.when((j >= 0) & (j < m) & (far < C - 1))
            def _():
                sl_copy(a, j).wait_recv()

                @pl.when(far > 0)
                def _():
                    sl_copy(a, j).start()
                for e in range(1, D):
                    xs_copy(a, j, e).start()
        return carry

    lax.fori_loop(0, n + skew * (C - 1), step, 0)

    def vt_copy(o):
        return copy(vt_own, vt_in.at[o - 1], vt_s.at[o - 1], vt_r.at[o - 1], row=(row + o) % R)

    def er_copy(x, a):
        c, d = plane[x]
        return copy(errs.at[dp, a], errs.at[dp, a], er_s.at[x], er_r.at[a, x],
                    col=(col + c) % C, dp=(dp + d) % D)

    def gh_copy(x, a):
        c, d = plane[x]
        return copy(gh.at[dp, a], gh.at[dp, a], gh_s.at[x], gh_r.at[a, x],
                    col=(col + c) % C, dp=(dp + d) % D)

    top = lax.broadcasted_iota(jnp.int32, (8, TB), 0)
    for a in range(2):
        @pl.when(col == (C - 1 if a == 0 else 0))
        def _():
            own = []
            for h in range(HI):
                seen = vals[h * TB:(h + 1) * TB, :] + tg_all[h * 2 + a][:, F + A:].astype(f32)
                own.append(seen.T[:8])
                vt_own[h] = own[h]
            for o in range(1, R):
                vt_copy(o).start()
            for o in range(1, R):
                vt_copy(o).wait()
            total = jnp.zeros((8, H), f32)
            for h in range(HI):
                summed = own[h]
                for o in range(1, R):
                    summed = summed + vt_in[o - 1, h]
                goal = own[h][4:5] + own[h][5:6] * jnp.minimum(summed[2:3], summed[3:4])
                err = jnp.where(top < 2, summed - goal, 0.0)
                errs[dp, a, h] = err
                twice = (2.0 * err).astype(bf16)
                for k in range(2):
                    got = jnp.dot(twice, hidden[k, h * TB:(h + 1) * TB, :],
                                  preferred_element_type=f32)
                    keep = lax.broadcasted_iota(jnp.int32, (8, H), 0) == k
                    total = total + jnp.where(keep, got, 0.0)
            for x in range(len(plane)):
                er_copy(x, a).start()
            gh[dp, a] = total
            for x in range(len(plane)):
                gh_copy(x, a).start()

    def late(s, carry):
        for a in range(2):
            far = col if a == 0 else C - 1 - col
            j = s - skew * (2 * (C - 1) - far)

            @pl.when((j >= 0) & (j < m) & (far < C - 1))
            def _():
                sl_copy(a, j).wait_recv()

                @pl.when(far > 0)
                def _():
                    sl_copy(a, j).start()
                for e in range(1, D):
                    xs_copy(a, j, e).start()
        return carry

    lax.fori_loop(n + skew * (C - 1), max(n + skew * (C - 1), m + 2 * skew * (C - 1)), late, 0)

    def pu_copy(o):
        return copy(pu_out.at[o], pu_in.at[o - 1], pu_s.at[o - 1], pu_r.at[o - 1],
                    row=(row + o) % R)

    def pz_copy(c):
        return copy(pz_all.at[col], pz_all.at[col], pz_s.at[c - 1], pz_r.at[c - 1],
                    col=(col + c) % C)

    lift = jnp.dot(a16[0], w16[0], preferred_element_type=f32).astype(bf16)
    last = (((1,), (1,)), ((), ()))
    first = (((0,), (0,)), ((), ()))
    own_push = None
    for o in range(R):
        got = lax.dot_general(slopes[0, rows_of(dp, (row + o) % R), :], lift, last,
                              preferred_element_type=f32)
        if o == 0:
            own_push = got
        else:
            pu_out[o] = got.astype(bf16)
            pu_copy(o).start()

    for e in range(1, D):
        src = (dp + D - e) % D
        for a in range(2):
            for o in range(HI):
                block = ((hi + o) % HI) * 2 + a
                xon_copy(a, o, block, e).wait_recv()
                embed_on(src, block)

    for o in range(1, R):
        pu_copy(o).wait_recv()
        own_push = own_push + pu_in[o - 1].astype(f32)
    pz_all[col] = own_push.astype(bf16)
    for c in range(1, C):
        pz_copy(c).start()

    for e in range(1, D):
        def take(j, carry):
            for a in range(2):
                xs_copy(a, j, e).wait_recv()
            return carry
        lax.fori_loop(0, m, take, 0)

    for a in range(2):
        end = C - 1 if a == 0 else 0
        for x, (c, d) in enumerate(plane):
            @pl.when((col + C - c) % C == end)
            def _():
                er_copy(x, a).wait_recv()

    epad[...] = jnp.zeros_like(epad)
    for d in range(D):
        for h in range(HI):
            for a in range(2):
                epad[0:8, :] = 2.0 * errs[d, a, h]
                column = epad[...].T
                at = slice((d * R + h * 2 + a) * TB, (d * R + h * 2 + a + 1) * TB)
                for k in range(2):
                    scaled = column[:, k:k + 1] * slopes[k, at, :].astype(f32)
                    delta[k, at, :] = scaled.astype(bf16)

    FR = F // R

    def ga_copy(o):
        to = (row + o) % R
        return copy(ga_out.at[to], ga_in.at[o - 1], ga_s.at[o - 1], ga_r.at[o - 1], row=to)

    def gb_copy(o):
        return copy(ga_all.at[row], ga_all.at[row], gb_s.at[o - 1], gb_r.at[o - 1],
                    row=(row + o) % R)

    for k in range(2):
        moved = jnp.zeros((A, H), f32)
        for d in range(D):
            for b in range(R):
                at = slice((d * R + b) * TB, (d * R + b + 1) * TB)
                moved = moved + lax.dot_general(on_all[d, b][:, F:], delta[k, at, :], first,
                                                preferred_element_type=f32)
        term = lax.dot_general(moved.astype(bf16), w16[k], last, preferred_element_type=f32)
        for p in range(R):
            piece = term[:, p * FR:(p + 1) * FR]
            ga_own[p, k] = piece
            ga_out[p, k] = piece.astype(bf16)
    for o in range(1, R):
        ga_copy(o).start()

    def grad_in(k):
        g_in[k] = jnp.zeros((F, H), f32)

        def add(d, carry):
            at = pl.ds(pl.multiple_of(d * R * TB, R * TB), R * TB)
            g_in[k] += lax.dot_general(emb[k, at, :], delta[k, at, :], first,
                                       preferred_element_type=f32)
            return carry
        lax.fori_loop(0, D, add, 0)

    grad_in(0)
    for o in range(1, R):
        ga_copy(o).wait_recv()
    for k in range(2):
        piece = ga_own[row, k]
        for o in range(1, R):
            piece = piece + ga_in[o - 1, k].astype(f32)
        ga_all[row, k] = piece.astype(bf16)
    for o in range(1, R):
        gb_copy(o).start()
    grad_in(1)

    for c in range(1, C):
        pz_copy(c).wait_recv()
    push = pz_all[0].astype(f32)
    for c in range(1, C):
        push = push + pz_all[c].astype(f32)
    push_out[...] = push
    errs_out[...] = errs[dp, lo, hi]

    for a in range(2):
        end = C - 1 if a == 0 else 0
        for x, (c, d) in enumerate(plane):
            @pl.when((col + C - c) % C == end)
            def _():
                gh_copy(x, a).wait_recv()
    whole = gh[0, 0]
    for d in range(D):
        for a in range(2):
            if d or a:
                whole = whole + gh[d, a]
    g_head[...] = whole

    for o in range(1, R):
        gb_copy(o).wait_recv()
    for p in range(R):
        for k in range(2):
            g_act[k, :, p * FR:(p + 1) * FR] = ga_all[p, k].astype(f32)

    for o in range(HI):
        on_copy(o).wait_send()
        tg_copy(o).wait_send()
        if o > 0:
            fon_copy(o, row).wait_send()
            ftg_copy(o, row).wait_send()
        for a in range(2):
            for e in range(1, D):
                xon_copy(a, o, row, e).wait_send()
    for a in range(2):
        far = col if a == 0 else C - 1 - col

        @pl.when(far < C - 1)
        def _():
            def left(i, carry):
                rs_copy(a, i).wait_send()
                return carry
            lax.fori_loop(0, n, left, 0)

        @pl.when(far > 0)
        def _():
            def left(j, carry):
                sl_copy(a, j).wait_send()
                return carry
            lax.fori_loop(0, m, left, 0)

        def gone(j, carry):
            for e in range(1, D):
                xs_copy(a, j, e).wait_send()
            return carry
        lax.fori_loop(0, m, gone, 0)

        @pl.when(far == C - 1)
        def _():
            for x in range(len(plane)):
                er_copy(x, a).wait_send()
                gh_copy(x, a).wait_send()
    for o in range(1, R):
        pu_copy(o).wait_send()
        ga_copy(o).wait_send()
        gb_copy(o).wait_send()
    for c in range(1, C):
        pz_copy(c).wait_send()


def on_device(dims, observed, next_observed, actions, next_mean, policy_noise, rewards, discounts,
              actor_flags, critic_in, critic_act, critic_head, target_in, target_act, target_head):
    R, C, D, TB, F, H, A = dims
    HI, TC = R // 2, TB // 2
    n, m, planes = 8 * HI, 4 * HI, C * D - 1
    noisy = jnp.clip(
        next_mean.astype(f32) + jnp.clip(policy_noise, -noise_clip, noise_clip), -1.0, 1.0
    ).astype(bf16)
    lanes = lax.broadcasted_iota(jnp.int32, (TB, 128), 1)
    zero = jnp.zeros((), bf16)
    extra = jnp.where(lanes == 4, rewards[:, None],
                      jnp.where(lanes == 5, discounts[:, None], zero))
    on_own = jnp.concatenate([observed, actions], axis=1)
    tg_own = jnp.concatenate([next_observed, noisy, extra], axis=1)
    heads = jnp.concatenate([critic_head, target_head], axis=0)[:, None, :]
    dma = lambda *shape: pltpu.SemaphoreType.DMA(shape)
    vmem = pltpu.VMEM
    scratch = [
        vmem((4, F, H), bf16), vmem((4, A, F), bf16),
        vmem((D, R, TB, F + A), bf16), vmem((R, TB, F + A + 128), bf16),
        vmem((2, (D + 1) * R * TB, F), bf16),
        vmem((2, D * R * TB, H), bf16), vmem((2, D * R * TB, H), bf16),
        vmem((2, n, TC, H), bf16), vmem((2, n, TC, H), bf16),
        vmem((2, HI * TB, H), bf16), vmem((HI * TB, 128), f32),
        vmem((HI, 8, TB), f32), vmem((R - 1, HI, 8, TB), f32),
        vmem((D, 2, HI, 8, TB), f32), vmem((D, 2, 8, H), f32), vmem((128, TB), f32),
        vmem((R, 2, A, F // R), f32), vmem((R, 2, A, F // R), bf16),
        vmem((R - 1, 2, A, F // R), bf16), vmem((R, 2, A, F // R), bf16),
        vmem((R, TB, A), bf16), vmem((R - 1, TB, A), bf16), vmem((C, TB, A), bf16),
        dma(HI), dma(HI), dma(HI), dma(HI),
        dma(HI), dma(HI), dma(HI), dma(HI),
        dma(2, HI, D - 1), dma(2, HI, D - 1),
        dma(2, n), dma(2, n), dma(2, m), dma(2, m),
        dma(2, m, D - 1), dma(2, m, D - 1),
        dma(R - 1), dma(R - 1),
        dma(planes), dma(2, planes), dma(planes), dma(2, planes),
        dma(R - 1), dma(R - 1), dma(R - 1), dma(R - 1),
        dma(R - 1), dma(R - 1), dma(C - 1), dma(C - 1),
    ]
    spec = pl.BlockSpec(memory_space=vmem)
    shaped = jax.ShapeDtypeStruct
    g_in, g_act, g_head, errors, push = pl.pallas_call(
        functools.partial(kernel, dims),
        out_shape=(shaped((2, F, H), f32), shaped((2, A, F), f32), shaped((8, H), f32),
                   shaped((8, TB), f32), shaped((TB, A), f32)),
        in_specs=[spec] * 7,
        out_specs=(spec,) * 5,
        scratch_shapes=scratch,
        compiler_params=pltpu.CompilerParams(
            collective_id=0, has_side_effects=True, vmem_limit_bytes=67043328),
    )(on_own, tg_own, critic_in, target_in, critic_act, target_act, heads)
    action_slope = push * actor_flags.astype(f32)[:, None]
    new_in = critic_in - matrix_rate * g_in
    new_act = critic_act - matrix_rate * g_act
    new_head = critic_head - head_rate * g_head[:2]
    new_target_in = blend_rate * new_in + (1.0 - blend_rate) * target_in
    new_target_act = blend_rate * new_act + (1.0 - blend_rate) * target_act
    new_target_head = blend_rate * new_head + (1.0 - blend_rate) * target_head
    return (new_in, new_act, new_head, new_target_in, new_target_act, new_target_head,
            errors[:2], action_slope)


def solution(mesh):
    def run(*args):
        R, C, D = mesh.shape["row"], mesh.shape["col"], mesh.shape["dp"]
        tokens, features = args[0].shape
        dims = (R, C, D, tokens // (R * D), features // C, args[8].shape[2] // R,
                args[2].shape[1])
        return sharded(dims)(*args)

    def sharded(dims):
        return jax.shard_map(
            functools.partial(on_device, dims),
            mesh=mesh,
            in_specs=(
                P(("row", "dp"), "col"),
                P(("row", "dp"), "col"),
                P(("row", "dp"), None),
                P(("row", "dp"), None),
                P(("row", "dp"), None),
                P(("row", "dp")),
                P(("row", "dp")),
                P(("row", "dp")),
                P(None, "col", "row"),
                P(None, None, "col"),
                P(None, "row"),
                P(None, "col", "row"),
                P(None, None, "col"),
                P(None, "row"),
            ),
            out_specs=(
                P(None, "col", "row"),
                P(None, None, "col"),
                P(None, "row"),
                P(None, "col", "row"),
                P(None, None, "col"),
                P(None, "row"),
                P(None, ("row", "dp")),
                P(("row", "dp"), None),
            ),
            check_vma=False,
        )

    return run
```

time: 339 us -> 97.4 us (0.29)
  waiting for transfers between devices: 157 us -> 0 us
  blocking collectives: 108 us -> 0 us
  Pallas kernels: 0 us -> 79.8 us
  matrix products: 31 us -> 0 us
  between operations: 14.4 us -> 0.72 us
  local copies, waits for them, and re-layouts: 9.12 us -> 1.88 us
    psum x3 -> x0, waiting for transfers between devices: 113 us -> none  [the longest x1 77.5 us: on_device(): lax.psum((grad_ins[0], grad_ins[1], grad_acts[0], grad_acts[1], head_grad...]
    all_gather x10 -> x0, blocking collectives: 87.6 us -> none  [the longest x1 21.9 us: on_device(): lax.all_gather(slopes[0], 'col', axis=0, tiled=True)]
    pallas_call x0 -> x1, Pallas kernels: none -> 79.8 us  [on_device(): pl.pallas_call(functools.partial(kernel, dims), out_shape=(shaped((2, F,...]
    reduce_scatter x4 -> x0, waiting for transfers between devices: 43.9 us -> none  [the longest x1 27.2 us: on_device(): lax.psum_scatter(partials[3], 'col', scatter_dimension=0, tiled=True)]
    dot_general x19 -> x0, matrix products: 31 us -> none  [the longest x4 8.82 us: contract_rows(): lax.dot_general(left, right, (((0,), (0,)), ((), ())), preferred_element_...]
    psum x3 -> x0, blocking collectives: 20.3 us -> none  [the longest x1 9.75 us: on_device(): head_grads = list(lax.psum((head_grads[0], head_grads[1]), 'col'))]
    another operation x6 -> x0, other arithmetic: 7.45 us -> none
    unnamed x61 -> x14, local copies, waits for them, and re-layouts: 6.54 us -> 0.03 us
  transfers between devices with their start and end apart: 7 -> 0, of which waited for: 6 -> 0; matrix products, arithmetic and copies ran while one was open for 11% -> 0% of each run, Pallas kernels for 0% -> 0%
where the time goes in v1:
time: 97.4 us; the launch traced here: 97.1 us
  Pallas kernels  79.8 us (82%)
  other arithmetic  14.7 us (15%)
  local copies, waits for them, and re-layouts  1.88 us (2%)
    pallas_call x1, Pallas kernels, on_device(): pl.pallas_call(functools.partial(kernel, dims), out_shape=(shaped((2, F,...  79.8 us
    add x1, other arithmetic, on_device(): new_target_in = blend_rate * new_in + (1.0 - blend_rate) * target_in  5.95 us

profile of v1, /device:TPU:1, one launch (start us, length us, event | category | flops | bytes accessed | tf_op | source)
XLA Modules:
  0.0 97.1 jit_solution(8129524342594419490)
XLA Ops:
  0.6 0.8 select_select_fusion
  1.4 0.9 clamp_convert_fusion
  2.3 1.6 %pad_maximum_fusion.tg_own = bf16[128,768]{1,0:T(8,128)(2,1)} fusion(bf16[128,128]{1,0:T(8,128)(2,1)S(1)} %select_select_fusion, bf16[128,128]{1,0:T(8,128)(2,1)S(1)} %clamp_convert_fusion, bf16[128,512]{1,0:T(8,128)(2,1)} %param.15), kind=kLoop, calls=%fused_computation.4 | loop fusion | flops 589824 | bytes 393216 | tf_op jit(solution)/shard_map/concatenate | solution.py:491
  3.9 1.6 %pad_maximum_fusion.1.on_own = bf16[128,640]{1,0:T(8,128)(2,1)} fusion(bf16[128,128]{1,0:T(8,128)(2,1)} %param.16, bf16[128,512]{1,0:T(8,128)(2,1)} %param.14), kind=kLoop, calls=%fused_computation.5 | loop fusion | flops 327680 | bytes 327680 | tf_op jit(solution)/shard_map/concatenate | solution.py:490
  5.5 0.7 pad_maximum_fusion.2
  6.2 0.6 broadcast_in_dim.29.heads
  6.8 79.8 %shard_map.197 = (f32[2,512,512]{2,1,0:T(8,128)}, f32[2,128,512]{2,1,0:T(8,128)}, f32[8,512]{1,0:T(8,128)}, f32[8,128]{1,0:T(8,128)}, f32[128,128]{1,0:T(8,128)}) custom-call(bf16[128,640]{1,0:T(8,128)(2,1)} %pad_maximum_fusion.1.on_own, bf16[128,768]{1,0:T(8,128)(2,1)} %pad_maximum_fusion.tg_own, f32[2,512,512]{2,1,0:T(8,128)} %cin.1, f32[2,512,512]{2,1,0:T(8,128)} %tin.1, ...), custom_call_target="tpu_custom_call" | custom-call | tf_op jit(solution)/shard_map/pallas_call | solution.py:519
  86.6 0.0 copy-start
  86.6 0.0 copy-start.1
  86.6 0.0 copy-start.2
  86.6 6.0 %multiply_add_fusion = (f32[2,512,512]{2,1,0:T(8,128)}, f32[2,512,512]{2,1,0:T(8,128)}) fusion(f32[2,512,512]{2,1,0:T(8,128)} %tin.1, f32[2,512,512]{2,1,0:T(8,128)} %cin.1, f32[2,512,512]{2,1,0:T(8,128)} %get-tuple-element.13), kind=kLoop, calls=%fused_computation | loop fusion | flops 2621440 | bytes 10485760 | tf_op jit(solution)/shard_map/add | solution.py:533
  92.6 0.0 copy-start.4
  92.6 0.0 copy-start.5
  92.6 0.0 copy-start.6
  92.6 0.0 copy-start.3
  92.6 0.0 copy-done
  92.6 0.0 copy-done.1
  92.6 0.0 copy-done.2
  92.6 1.1 %multiply_add_fusion.1 = (f32[2,128,512]{2,1,0:T(8,128)}, f32[2,128,512]{2,1,0:T(8,128)}) fusion(f32[2,128,512]{2,1,0:T(8,128)S(1)} %copy-done.1, f32[2,128,512]{2,1,0:T(8,128)S(1)} %copy-done, f32[2,128,512]{2,1,0:T(8,128)S(1)} %copy-done.2), kind=kLoop, calls=%fused_computation.2 | loop fusion | flops 655360 | bytes 2621440 | tf_op jit(solution)/shard_map/add | solution.py:534
  93.8 0.0 copy-done.4
  93.8 0.0 copy-done.5
  93.8 1.3 %multiply_add_fusion.2 = (f32[2,512]{1,0:T(2,128)}, f32[2,512]{1,0:T(2,128)}) fusion(f32[2,512]{1,0:T(2,128)S(1)} %copy-done.4, f32[2,512]{1,0:T(2,128)S(1)} %copy-done.5, f32[8,512]{1,0:T(8,128)} %get-tuple-element.15), kind=kLoop, calls=%fused_computation.10 | loop fusion | flops 5120 | bytes 20480 | tf_op jit(solution)/shard_map/add | solution.py:535
  95.1 0.0 copy-done.6
  95.1 0.0 copy-done.3
  95.1 0.7 broadcast_multiply_fusion
  95.8 1.2 %slice.7 = f32[2,128]{1,0:T(2,128)} slice(f32[8,128]{1,0:T(8,128)} %get-tuple-element.16), slice={[0:2], [0:128]} | slice | bytes 2048 | tf_op jit(solution)/shard_map/slice | solution.py:537
  (2 shorter events, 0.0 us)
Async XLA Ops:
  86.6 6.0 %copy-start = (f32[2,128,512]{2,1,0:T(8,128)S(1)}, f32[2,128,512]{2,1,0:T(8,128)}, u32[]{:S(2)}) copy-start(f32[2,128,512]{2,1,0:T(8,128)} %cact.1) | copy-start | bytes 1572868
  86.6 6.0 %copy-start.1 = (f32[2,128,512]{2,1,0:T(8,128)S(1)}, f32[2,128,512]{2,1,0:T(8,128)}, u32[]{:S(2)}) copy-start(f32[2,128,512]{2,1,0:T(8,128)} %tact.1) | copy-start | bytes 1572868
  86.6 6.0 %copy-start.2 = (f32[2,128,512]{2,1,0:T(8,128)S(1)}, f32[2,128,512]{2,1,0:T(8,128)}, u32[]{:S(2)}) copy-start(f32[2,128,512]{2,1,0:T(8,128)} %get-tuple-element.14) | copy-start | bytes 1572868
  92.6 1.2 %copy-start.4 = (f32[2,512]{1,0:T(2,128)S(1)}, f32[2,512]{1,0:T(2,128)}, u32[]{:S(2)}) copy-start(f32[2,512]{1,0:T(2,128)} %param.27) | copy-start | bytes 12292
  92.6 1.2 %copy-start.5 = (f32[2,512]{1,0:T(2,128)S(1)}, f32[2,512]{1,0:T(2,128)}, u32[]{:S(2)}) copy-start(f32[2,512]{1,0:T(2,128)} %param.24) | copy-start | bytes 12292
  92.6 2.5 %copy-start.6 = (s32[128]{0:T(128)S(1)}, s32[128]{0:T(128)}, u32[]{:S(2)}) copy-start(s32[128]{0:T(128)} %param.21) | copy-start | bytes 1540
  92.6 2.5 %copy-start.3 = (f32[128,128]{1,0:T(8,128)S(1)}, f32[128,128]{1,0:T(8,128)}, u32[]{:S(2)}) copy-start(f32[128,128]{1,0:T(8,128)} %get-tuple-element.17) | copy-start | bytes 196612

commit v2 on v1

--- a/solution.py
+++ b/solution.py
@@ -14,10 +14,12 @@
 
 f32 = jnp.float32
 bf16 = jnp.bfloat16
-skew = 3
-
-
-def kernel(dims, on_own, tg_own, cin, tin, cact, tact, heads, g_in, g_act, g_head, errs_out, push_out,
+skew = 2
+
+
+def kernel(dims, observed, next_observed, actions, next_mean, noise, rewards, discounts, flags,
+           cin, cact, chead, tin, tact, thead, new_in, new_act, new_head, new_tin, new_tact,
+           new_thead, errs_out, push_out, on_own, tg_own, heads, flag_column, columns,
            w16, a16, on_all, tg_all, emb, slopes, delta, rs_out, rs_in, hidden, vals, vt_own, vt_in,
            errs, gh, epad, ga_own, ga_out, ga_in, ga_all, pu_out, pu_in, pz_all,
            on_s, on_r, tg_s, tg_r, fon_s, fon_r, ftg_s, ftg_r, xon_s, xon_r,
@@ -35,6 +37,22 @@
         return pltpu.make_async_remote_copy(
             src_ref=src, dst_ref=dst, send_sem=ssem, recv_sem=rsem,
             device_id=where, device_id_type=pl.DeviceIdType.MESH)
+
+    on_own[:, :F] = observed[...]
+    on_own[:, F:] = actions[...]
+    tg_own[:, :F] = next_observed[...]
+    tg_own[:, F:F + A] = jnp.clip(
+        next_mean[...].astype(f32) + jnp.clip(noise[...], -noise_clip, noise_clip), -1.0, 1.0
+    ).astype(bf16)
+    epad[...] = jnp.zeros_like(epad)
+    epad[4:5, :] = rewards[...].astype(f32)
+    epad[5:6, :] = discounts[...].astype(f32)
+    tg_own[:, F + A:] = epad[...].T.astype(bf16)
+    epad[0:1, :] = flags[...].astype(f32)
+    flag_column[...] = epad[...].T[:, 0:1]
+    for k in range(2):
+        heads[k] = chead[k:k + 1, :]
+        heads[2 + k] = thead[k:k + 1, :]
 
     plane = [(c, d) for d in range(D) for c in range(C) if c or d]
     barrier = pltpu.get_barrier_semaphore()
@@ -350,11 +368,8 @@
         for h in range(HI):
             for a in range(2):
                 epad[0:8, :] = 2.0 * errs[d, a, h]
-                column = epad[...].T
                 at = slice((d * R + h * 2 + a) * TB, (d * R + h * 2 + a + 1) * TB)
-                for k in range(2):
-                    scaled = column[:, k:k + 1] * slopes[k, at, :].astype(f32)
-                    delta[k, at, :] = scaled.astype(bf16)
+                columns[at, :] = epad[...].T
 
     FR = F // R
 
@@ -371,7 +386,8 @@
         for d in range(D):
             for b in range(R):
                 at = slice((d * R + b) * TB, (d * R + b + 1) * TB)
-                moved = moved + lax.dot_general(on_all[d, b][:, F:], delta[k, at, :], first,
+                scaled = columns[at, k:k + 1] * on_all[d, b][:, F:].astype(f32)
+                moved = moved + lax.dot_general(scaled.astype(bf16), slopes[k, at, :], first,
                                                 preferred_element_type=f32)
         term = lax.dot_general(moved.astype(bf16), w16[k], last, preferred_element_type=f32)
         for p in range(R):
@@ -381,15 +397,26 @@
     for o in range(1, R):
         ga_copy(o).start()
 
+    def blend(fresh, target):
+        return blend_rate * fresh + (1.0 - blend_rate) * target
+
     def grad_in(k):
-        g_in[k] = jnp.zeros((F, H), f32)
+        for b in range(D * R):
+            at = slice(b * TB, (b + 1) * TB)
+            scaled = columns[at, k:k + 1] * slopes[k, at, :].astype(f32)
+            delta[k, at, :] = scaled.astype(bf16)
 
         def add(d, carry):
             at = pl.ds(pl.multiple_of(d * R * TB, R * TB), R * TB)
-            g_in[k] += lax.dot_general(emb[k, at, :], delta[k, at, :], first,
-                                       preferred_element_type=f32)
+            new_in[k] += lax.dot_general(emb[k, at, :], delta[k, at, :], first,
+                                         preferred_element_type=f32)
             return carry
-        lax.fori_loop(0, D, add, 0)
+        new_in[k] = lax.dot_general(emb[k, :R * TB, :], delta[k, :R * TB, :], first,
+                                    preferred_element_type=f32)
+        lax.fori_loop(1, D, add, 0)
+        fresh = cin[k] - matrix_rate * new_in[k]
+        new_in[k] = fresh
+        new_tin[k] = blend(fresh, tin[k])
 
     grad_in(0)
     for o in range(1, R):
@@ -408,8 +435,8 @@
     push = pz_all[0].astype(f32)
     for c in range(1, C):
         push = push + pz_all[c].astype(f32)
-    push_out[...] = push
-    errs_out[...] = errs[dp, lo, hi]
+    push_out[...] = push * flag_column[...]
+    errs_out[...] = errs[dp, lo, hi, 0:2, :]
 
     for a in range(2):
         end = C - 1 if a == 0 else 0
@@ -422,13 +449,17 @@
         for a in range(2):
             if d or a:
                 whole = whole + gh[d, a]
-    g_head[...] = whole
+    new_head[...] = chead[...] - head_rate * whole[:2]
+    new_thead[...] = blend(new_head[...], thead[...])
 
     for o in range(1, R):
         gb_copy(o).wait_recv()
     for p in range(R):
         for k in range(2):
-            g_act[k, :, p * FR:(p + 1) * FR] = ga_all[p, k].astype(f32)
+            part = slice(p * FR, (p + 1) * FR)
+            fresh = cact[k, :, part] - matrix_rate * ga_all[p, k].astype(f32)
+            new_act[k, :, part] = fresh
+            new_tact[k, :, part] = blend(fresh, tact[k, :, part])
 
     for o in range(HI):
         on_copy(o).wait_send()
@@ -480,19 +511,11 @@
     R, C, D, TB, F, H, A = dims
     HI, TC = R // 2, TB // 2
     n, m, planes = 8 * HI, 4 * HI, C * D - 1
-    noisy = jnp.clip(
-        next_mean.astype(f32) + jnp.clip(policy_noise, -noise_clip, noise_clip), -1.0, 1.0
-    ).astype(bf16)
-    lanes = lax.broadcasted_iota(jnp.int32, (TB, 128), 1)
-    zero = jnp.zeros((), bf16)
-    extra = jnp.where(lanes == 4, rewards[:, None],
-                      jnp.where(lanes == 5, discounts[:, None], zero))
-    on_own = jnp.concatenate([observed, actions], axis=1)
-    tg_own = jnp.concatenate([next_observed, noisy, extra], axis=1)
-    heads = jnp.concatenate([critic_head, target_head], axis=0)[:, None, :]
     dma = lambda *shape: pltpu.SemaphoreType.DMA(shape)
     vmem = pltpu.VMEM
     scratch = [
+        vmem((TB, F + A), bf16), vmem((TB, F + A + 128), bf16), vmem((4, 1, H), f32),
+        vmem((TB, 1), f32), vmem((D * R * TB, 128), f32),
         vmem((4, F, H), bf16), vmem((4, A, F), bf16),
         vmem((D, R, TB, F + A), bf16), vmem((R, TB, F + A + 128), bf16),
         vmem((2, (D + 1) * R * TB, F), bf16),
@@ -516,25 +539,19 @@
     ]
     spec = pl.BlockSpec(memory_space=vmem)
     shaped = jax.ShapeDtypeStruct
-    g_in, g_act, g_head, errors, push = pl.pallas_call(
+    return pl.pallas_call(
         functools.partial(kernel, dims),
-        out_shape=(shaped((2, F, H), f32), shaped((2, A, F), f32), shaped((8, H), f32),
-                   shaped((8, TB), f32), shaped((TB, A), f32)),
-        in_specs=[spec] * 7,
-        out_specs=(spec,) * 5,
+        out_shape=(shaped((2, F, H), f32), shaped((2, A, F), f32), shaped((2, H), f32),
+                   shaped((2, F, H), f32), shaped((2, A, F), f32), shaped((2, H), f32),
+                   shaped((2, TB), f32), shaped((TB, A), f32)),
+        in_specs=[spec] * 14,
+        out_specs=(spec,) * 8,
         scratch_shapes=scratch,
         compiler_params=pltpu.CompilerParams(
             collective_id=0, has_side_effects=True, vmem_limit_bytes=67043328),
-    )(on_own, tg_own, critic_in, target_in, critic_act, target_act, heads)
-    action_slope = push * actor_flags.astype(f32)[:, None]
-    new_in = critic_in - matrix_rate * g_in
-    new_act = critic_act - matrix_rate * g_act
-    new_head = critic_head - head_rate * g_head[:2]
-    new_target_in = blend_rate * new_in + (1.0 - blend_rate) * target_in
-    new_target_act = blend_rate * new_act + (1.0 - blend_rate) * target_act
-    new_target_head = blend_rate * new_head + (1.0 - blend_rate) * target_head
-    return (new_in, new_act, new_head, new_target_in, new_target_act, new_target_head,
-            errors[:2], action_slope)
+    )(observed, next_observed, actions, next_mean, policy_noise, rewards[None, :],
+      discounts[None, :], actor_flags[None, :], critic_in, critic_act, critic_head, target_in,
+      target_act, target_head)
 
 
 def solution(mesh):

time: 97.4 us -> 89.5 us (0.919)
  other arithmetic: 14.7 us -> 0 us
  local copies, waits for them, and re-layouts: 1.88 us -> 8.55 us
    unnamed x14 -> x22, local copies, waits for them, and re-layouts: 0.03 us -> 8.55 us
    add x3 -> x0, other arithmetic: 8.42 us -> none  [the longest x1 5.95 us: on_device(): new_target_in = blend_rate * new_in + (1.0 - blend_rate) * target_in]
    concatenate x3 -> x0, other arithmetic: 3.92 us -> none  [the longest x1 1.6 us: on_device(): on_own = jnp.concatenate([observed, actions], axis=1)]
    slice x1 -> x0, local copies, waits for them, and re-layouts: 1.24 us -> none  [on_device(): errors[:2]]
where the time goes in v2:
time: 89.5 us; the launch traced here: 89.3 us
  Pallas kernels  80.1 us (89%)
  local copies, waits for them, and re-layouts  8.55 us (10%)
    pallas_call x1, Pallas kernels, on_device(): pl.pallas_call(functools.partial(kernel, dims), out_shape=(shaped((2, F,...  80.1 us
    unnamed x22, local copies, waits for them, and re-layouts  8.55 us

profile of v2, /device:TPU:1, one launch (start us, length us, event | category | flops | bytes accessed | tf_op | source)
XLA Modules:
  0.0 89.3 jit_solution(7763442560759126825)
XLA Ops:
  0.6 80.1 %shard_map.197 = (f32[2,512,512]{2,1,0:T(8,128)}, f32[2,128,512]{2,1,0:T(8,128)}, f32[2,512]{1,0:T(2,128)}, f32[2,512,512]{2,1,0:T(8,128)}, f32[2,128,512]{2,1,0...) custom-call(bf16[128,512]{1,0:T(8,128)(2,1)} %observed.1, bf16[128,512]{1,0:T(8,128)(2,1)} %next_observed.1, ...), custom_call_target="tpu_custom_call" | custom-call | tf_op jit(solution)/shard_map/pallas_call | solution.py:542
  80.7 0.0 copy-start.2
  80.7 0.0 copy-start.5
  80.7 0.0 copy-start
  80.7 3.2 %copy.30 = f32[2,512,512]{2,1,0:T(8,128)} copy(f32[2,512,512]{2,1,0:T(8,128)} %get-tuple-element.16) | data formatting | bytes 4194304
  84.0 0.0 copy-done.2
  84.0 0.8 copy.31
  84.8 0.0 copy-done.5
  84.8 0.6 copy.32
  85.4 0.0 copy-done
  85.4 0.0 copy-start.1
  85.4 0.0 copy-start.4
  85.4 0.0 copy-start.6
  85.4 0.0 copy-start.3
  85.4 1.3 %copy.33 = f32[2,512,512]{2,1,0:T(8,128)} copy(f32[2,512,512]{2,1,0:T(8,128)S(1)} %copy-done) | data formatting | bytes 4194304
  86.7 0.0 copy-done.1
  86.7 0.8 copy.34
  87.5 0.0 copy-done.4
  87.5 0.6 copy.35
  88.1 0.0 copy-done.6
  88.1 0.6 copy.36
  88.7 0.0 copy-done.3
  88.7 0.6 copy.37
Async XLA Ops:
  80.7 3.3 %copy-start.2 = (f32[2,128,512]{2,1,0:T(8,128)S(1)}, f32[2,128,512]{2,1,0:T(8,128)}, u32[]{:S(2)}) copy-start(f32[2,128,512]{2,1,0:T(8,128)} %get-tuple-element.17) | copy-start | bytes 1572868
  80.7 4.0 %copy-start.5 = (f32[2,512]{1,0:T(2,128)S(1)}, f32[2,512]{1,0:T(2,128)}, u32[]{:S(2)}) copy-start(f32[2,512]{1,0:T(2,128)} %get-tuple-element.18) | copy-start | bytes 12292
  80.7 4.6 %copy-start = (f32[2,512,512]{2,1,0:T(8,128)S(1)}, f32[2,512,512]{2,1,0:T(8,128)}, u32[]{:S(2)}) copy-start(f32[2,512,512]{2,1,0:T(8,128)} %get-tuple-element.19) | copy-start | bytes 6291460
  85.4 1.4 %copy-start.1 = (f32[2,128,512]{2,1,0:T(8,128)S(1)}, f32[2,128,512]{2,1,0:T(8,128)}, u32[]{:S(2)}) copy-start(f32[2,128,512]{2,1,0:T(8,128)} %get-tuple-element.20) | copy-start | bytes 1572868
  85.4 2.1 %copy-start.4 = (f32[2,512]{1,0:T(2,128)S(1)}, f32[2,512]{1,0:T(2,128)}, u32[]{:S(2)}) copy-start(f32[2,512]{1,0:T(2,128)} %get-tuple-element.21) | copy-start | bytes 12292
  85.4 2.7 %copy-start.6 = (f32[2,128]{1,0:T(2,128)S(1)}, f32[2,128]{1,0:T(2,128)}, u32[]{:S(2)}) copy-start(f32[2,128]{1,0:T(2,128)} %get-tuple-element.22) | copy-start | bytes 3076
  85.4 3.3 %copy-start.3 = (f32[128,128]{1,0:T(8,128)S(1)}, f32[128,128]{1,0:T(8,128)}, u32[]{:S(2)}) copy-start(f32[128,128]{1,0:T(8,128)} %get-tuple-element.23) | copy-start | bytes 196612
